TPU v7x, 32 devices: a whole 2x2x4 slice. The times are simulated.
32 devices in a mesh: front: 4 (over x, core), grid: 8 (over z, y).
Axes of the slice: x: 2, y: 2, z: 4, core: 2. Of those that a mesh axis runs over, the one named last changes fastest.
Arguments:
- index_map: int32 [4, 8192], P('front'), may hold values from 0 to 16383, as said below
- lengths: int32 [4], P('front'), may hold values from 1 to 8192, 24576 in all
- update_front: float32 [4, 8192, 8192], P('front', 'grid'), may hold values from -0.0625 to 0.0625
- front_matrix: float32 [16384, 16384], P(('front', 'grid')), may hold values from -0.046875 to 0.046875
- random: float32 [16384, 256], P(('front', 'grid')), may hold values from -6 to 6
Outputs:
- parent_sample: float32 [16384, 256], P(('front', 'grid'))
Inputs may be any that keep to these rules, and one draw needn't show every extreme that they name: `index_map`: within one child the 8192 entries are distinct parent rows. `lengths`: rows of a child at or past its length are not live; the largest length equals 8192.
All inputs are finite; a program needn't handle non-finite values. No bound on the sum of `lengths` on one device may be relied on, other than what follows from the above.
Results may differ from a plain program's by a relative error of at most 0.0003.
Values sent between devices are 32-bit elements; how exact they have to be, the bound alone decides.
A program may use at most 192 MiB of HBM per device.

v0:
```python
import jax
import jax.numpy as jnp
from jax import lax
from jax.sharding import PartitionSpec as P


def product(a, b):
    return jnp.dot(a, b, preferred_element_type=jnp.float32, precision=lax.Precision.HIGH)


def shards(index_map, lengths, update_front, front_matrix, random):
    gathered_random = lax.all_gather(random, ("front", "grid"), axis=0, tiled=True)
    own_rows = front_matrix.shape[0]
    half = own_rows // 2
    index_rows = index_map[0]
    child_random = jnp.take(gathered_random, index_rows, axis=0)
    child_sample = product(update_front[0], child_random)
    local_rows = child_sample.shape[0]
    first_row = lax.axis_index("grid") * local_rows
    row_numbers = first_row + jnp.arange(local_rows, dtype=jnp.int32)
    live_rows = row_numbers < lengths[0]
    child_sample = jnp.where(live_rows[:, None], child_sample, jnp.float32(0.0))
    child_sample, gathered_random = lax.optimization_barrier((child_sample, gathered_random))
    group_sample = lax.all_gather(child_sample, "grid", axis=0, tiled=True)
    upper = product(front_matrix[:half], gathered_random)
    group_sample, upper = lax.optimization_barrier((group_sample, upper))
    group_count = lax.axis_size("front")
    grid_count = lax.axis_size("grid")
    grid_place = lax.axis_index("grid")
    block_ids = jnp.arange(group_count, dtype=jnp.int32)[:, None] * grid_count + grid_place
    targets = (block_ids * own_rows + jnp.arange(own_rows, dtype=jnp.int32)[None, :]).reshape(-1)
    one_hot = (targets[:, None] == index_rows[None, :]).astype(jnp.bfloat16)
    coarse = lax.reduce_precision(group_sample, 8, 7)
    rest = group_sample - coarse
    halves = jnp.concatenate([coarse, rest], axis=1).astype(jnp.bfloat16)
    both = jnp.dot(one_hot, halves, preferred_element_type=jnp.float32)
    width = group_sample.shape[1]
    terms = both[:, :width] + both[:, width:]
    terms = terms.reshape(group_count, own_rows, width)
    terms, gathered_random = lax.optimization_barrier((terms, gathered_random))
    added = lax.psum_scatter(terms, "front", scatter_dimension=0, tiled=True)[0]
    lower = product(front_matrix[half:], gathered_random)
    added, lower = lax.optimization_barrier((added, lower))
    return jnp.concatenate([upper, lower], axis=0) + added


def solution(mesh):
    placed = (
        P("front", None),
        P("front"),
        P("front", "grid", None),
        P(("front", "grid"), None),
        P(("front", "grid"), None),
    )
    return jax.shard_map(
        shards, mesh=mesh, in_specs=placed, out_specs=P(("front", "grid"), None), check_vma=False
    )
```

profile of v0, /device:TPU:0, one launch (start us, length us, event | category | flops | bytes accessed | tf_op | source)
XLA Modules:
  0.0 391.2 jit_solution(2507641239275346115)
XLA Ops:
  6.5 0.0 all-gather.3.cloned.1.call-start
  6.5 0.7 all-gather.3.cloned.1.call-update
  7.3 0.0 all-gather.5.cloned.1.call-start
  8.0 0.8 compare_and_fusion
  8.7 0.8 compare_select_fusion
  9.6 118.0 %all-gather.3.cloned.1.call-done = f32[16384,256]{1,0:T(8,128)} async-done(((f32[512,256]{1,0:T(8,128)}), f32[16384,256]{1,0:T(8,128)}) %all-gather.3.cloned.1.call-update) | async-done | bytes 16777232 | tf_op jit(solution)/shard_map/all_gather | solution.py:12
  127.5 37.3 %gather_fusion = f32[8192,256]{1,0:T(8,128)} fusion(f32[16384,256]{1,0:T(8,128)} %all-gather.3.cloned.1.call-done, s32[8192]{0:T(1024)S(1)} %broadcast_clamp_fusion), kind=kCustom, calls=%fused_computation | custom fusion | bytes 16809984 | tf_op jit(solution)/shard_map/jit(_take)/gather | solution.py:16
  164.8 33.2 %fusion.22 = f32[1024,256]{0,1:T(8,128)} fusion(f32[1,1024,8192]{2,1,0:T(8,128)} %param.7, f32[8192,256]{1,0:T(8,128)} %gather_fusion, pred[8192]{0:T(1024)(128)(4,1)S(1)} %compare_and_fusion, pred[1024]{0:T(1024)(128)(4,1)S(1)} %add_compare_fusion), kind=kOutput, calls=%fused_computation.22 | convolution fusion | flops 12887261184 | bytes 43000832 | tf_op jit(solution)/shard_map/dot_general | solution.py:8
  198.0 0.0 all-gather.5.cloned.1.call-update
  198.1 0.2 reduce-scatter.2.cloned.1.call-start
  198.3 0.1 add_bitcast_fusion
  198.4 22.6 %fusion.27 = f32[256,256]{0,1:T(8,128)S(1)} fusion(f32[16384,256]{1,0:T(8,128)} %all-gather.3.cloned.1.call-done, f32[512,16384]{1,0:T(8,128)} %param.8), kind=kOutput, calls=%fused_computation.23 | convolution fusion | flops 6442450944 | bytes 33816576 | tf_op jit(solution)/shard_map/dot_general | solution.py:8
  221.0 0.0 copy-start
  221.0 99.9 %all-gather.5.cloned.1.call-done = f32[8192,256]{0,1:T(8,128)} async-done(((f32[1024,256]{0,1:T(8,128)}), f32[8192,256]{0,1:T(8,128)}) %all-gather.5.cloned.1.call-update) | async-done | bytes 8388624 | tf_op jit(solution)/shard_map/all_gather | solution.py:24
  320.9 8.1 %reduce-precision_convert_fusion = (bf16[8192,256]{0,1:T(8,128)(2,1)}, bf16[8192,256]{0,1:T(8,128)(2,1)}) fusion(f32[8192,256]{0,1:T(8,128)} %all-gather.5.cloned.1.call-done), kind=kLoop, calls=%fused_computation.12 | loop fusion | flops 8388608 | bytes 16777216 | tf_op jit(solution)/shard_map/convert
  329.1 0.0 copy-done
  329.1 21.8 %fusion = f32[2048,512]{1,0:T(8,128)S(1)} fusion(s32[8192]{0:T(1024)S(1)} %bitcast.29, s32[2048]{0:T(1024)S(1)} %bitcast.31, bf16[8192,256]{0,1:T(8,128)(2,1)} %get-tuple-element.22, bf16[8192,256]{0,1:T(8,128)(2,1)} %get-tuple-element.21), kind=kOutput, calls=%fused_computation.1 | convolution fusion | flops 17213423616 | bytes 12623872 | tf_op jit(solution)/shard_map/dot_general | solution.py:36
  350.9 0.3 slice_add_fusion
  351.2 1.9 copy.7
  353.1 0.0 reduce-scatter.2.cloned.1.call-update
  353.1 22.6 %fusion.30 = f32[256,256]{0,1:T(8,128)S(1)} fusion(f32[16384,256]{1,0:T(8,128)} %all-gather.3.cloned.1.call-done, f32[512,16384]{1,0:T(8,128)} %param.8), kind=kOutput, calls=%fused_computation.24 | convolution fusion | flops 6442450944 | bytes 33816576 | tf_op jit(solution)/shard_map/dot_general | solution.py:8
  375.7 6.9 %reduce-scatter.2.cloned.1.call-done = f32[1,512,256]{1,2,0:T(8,128)} async-done(((f32[4,512,256]{1,2,0:T(8,128)}), f32[1,512,256]{1,2,0:T(8,128)}) %reduce-scatter.2.cloned.1.call-update) | async-done | bytes 524304 | tf_op jit(solution)/shard_map/reduce_scatter | solution.py:41
  382.6 1.1 maximum_add_fusion
  383.7 1.0 copy.8
  (4 shorter events, 0.0 us)
Async XLA Ops:
  6.5 121.0 %all-gather.3.cloned.1.call-start = ((), (), s32[]{:S(2)}) async-start(), calls=%async_computation.1 | async-start | bytes 17301504 | tf_op jit(solution)/shard_map/all_gather | solution.py:12
  7.3 313.7 %all-gather.5.cloned.1.call-start = ((), (), s32[]{:S(2)}) async-start(), calls=%async_computation.2 | async-start | bytes 9437184 | tf_op jit(solution)/shard_map/all_gather | solution.py:24
  198.1 184.5 %reduce-scatter.2.cloned.1.call-start = ((), (), s32[]{:S(2)}) async-start(), calls=%async_computation.3 | async-start | bytes 2621440 | tf_op jit(solution)/shard_map/reduce_scatter | solution.py:41
  221.0 108.1 %copy-start = (s32[1,8192]{1,0:T(1,128)S(1)}, s32[1,8192]{1,0:T(1,128)}, u32[]{:S(2)}) copy-start(s32[1,8192]{1,0:T(1,128)} %param.5) | copy-start | bytes 98308
Sparse Core Ops, SparseCore 0:
  10.4 117.0 all-gather.2
  198.2 122.6 all-gather.4
  353.2 29.3 reduce-scatter.1
where the time goes:
time: 392 us; the launch traced here: 391 us
  waiting for transfers between devices  226 us (58%)
  matrix products  100 us (26%)
  local copies, waits for them, and re-layouts  40.2 us (10%)
  between operations  13.8 us (4%)
  other arithmetic  11.2 us (3%)
    all_gather x1, waiting for transfers between devices, shards(): lax.all_gather(random, ('front', 'grid'), axis=0, tiled=True)  118 us
    all_gather x1, waiting for transfers between devices, shards(): group_sample = lax.all_gather(child_sample, 'grid', axis=0, tiled=True)  99.9 us
    dot_general x3, matrix products, product(): jnp.dot(a, b, preferred_element_type=jnp.float32, precision=lax.Precision...  78.4 us
    gather x1, local copies, waits for them, and re-layouts, shards(): child_random = jnp.take(gathered_random, index_rows, axis=0)  37.3 us
    dot_general x1, matrix products, shards(): both = jnp.dot(one_hot, halves, preferred_element_type=jnp.float32)  21.8 us
    another operation x1, other arithmetic  8.15 us
  transfers between devices with their start and end apart: 3, of which 3 were waited for; matrix products, arithmetic and copies ran while one was open for 12% of the time, Pallas kernels for 0%

commit v1 on v0

v1 whole, which is shorter than its diff:
```python
import functools
import itertools
import math

import jax
import jax.numpy as jnp
from jax import lax
from jax.experimental import pallas as pl
from jax.experimental.pallas import tpu as pltpu
from jax.sharding import PartitionSpec as P

MESH = pl.DeviceIdType.MESH


def axis_dims(places):
    found = []
    for d in range(len(places[0])):
        values = [p[d] for p in places]
        size = len(set(values))
        if size > 1:
            stride = next(i for i, v in enumerate(values) if v != values[0])
            found.append((stride, size))
    found.sort(reverse=True)
    if math.prod(size for _, size in found) != len(places):
        found = [(1, len(places))]
    return found


class Plan:
    def __init__(self, mesh):
        self.front, self.grid = mesh.shape["front"], mesh.shape["grid"]
        place = lambda d: (*d.coords, d.core_on_chip)
        fronts = axis_dims([place(d) for d in mesh.devices[:, 0]])
        grids = axis_dims([place(d) for d in mesh.devices[0, :]])
        self.core = fronts[-1] if fronts[-1][1] == 2 else (1, 1)
        if self.core[1] == 2:
            fronts = fronts[:-1]
        dims = [("front", s, n) for s, n in fronts] + [("grid", s, n) for s, n in grids]
        long = max(range(len(dims)), key=lambda i: dims[i][2])
        rest = [i for i in range(len(dims)) if i != long]
        self.dims = dims
        a, b = rest, rest[::-1]
        if len(rest) == 2:
            self.orders = [(a[0], long, a[1]), (b[0], long, b[1]), (long, *a), (long, *b)]
        else:
            self.orders = [(*a, long), (long, *b)]
        self.items = self.schedule()

    def steps(self, offset, order):
        last = max((i for i, d in enumerate(order) if offset[d]), default=-1)
        moves = []
        if last >= 0 and self.dims[order[last]][2] > 2:
            moves.append((order[last], 1 if offset[order[last]] > 0 else -1))
        for d in order[last + 1 :]:
            moves += [(d, 1)] if self.dims[d][2] == 2 else [(d, 1), (d, -1)]
        return moves

    def schedule(self):
        spans = [range(2) if n == 2 else range(1 - n, n) for _, _, n in self.dims]
        items = []
        for offset in itertools.product(*spans):
            for color, order in enumerate(self.orders):
                stage = max((i for i, d in enumerate(order) if offset[d]), default=-1)
                items.append((sum(map(abs, offset)), stage, color, offset))
        items.sort()
        return [(color, offset) for hops, _, color, offset in items if hops]


def gather_rows(plan, x_ref, buf, own_sem, send, side_send, recv, side_recv, between=lambda: None):
    f, g = lax.axis_index("front"), lax.axis_index("grid")
    rows = x_ref.shape[0]
    colors = len(plan.orders)
    part = rows // colors
    at = [lax.rem((f if axis == "front" else g) // s, n) for axis, s, n in plan.dims]
    sibling = (f + 1 - 2 * lax.rem(f, 2), g)

    def moved(d, step):
        axis, stride, n = plan.dims[d]
        move = (1 - 2 * at[d]) if n == 2 else step
        return (f + move * stride, g) if axis == "front" else (f, g + move * stride)

    def inside(d, step):
        n = plan.dims[d][2]
        if n == 2:
            return None
        return at[d] + step <= n - 1 if step > 0 else at[d] + step >= 0

    def guarded(conditions, body):
        conditions = [c for c in conditions if c is not None]
        if conditions:
            pl.when(functools.reduce(jnp.logical_and, conditions))(body)
        else:
            body()

    def piece(ref, first, color):
        return ref.at[pl.ds(pl.multiple_of(first + color * part, 8), part)]

    def lane(d, step):
        return 2 * d + (step < 0)

    def remote(source, target, first, color, send_sem, recv_sem, device):
        return pltpu.make_async_remote_copy(
            src_ref=source, dst_ref=piece(target, first, color), send_sem=send_sem, recv_sem=recv_sem,
            device_id=device, device_id_type=MESH,
        )

    me = f * plan.grid + g
    seat = lambda ff, gg: (ff // plan.core[1]) * plan.grid + gg

    def pass_on(color, source, owner_f, owner_g, moves, conditions):
        first = (owner_f * plan.grid + owner_g) * rows
        for d, step in moves:
            def go(d=d, step=step):
                remote(
                    source, buf, first, color, send.at[lane(d, step), color, seat(owner_f, owner_g)],
                    recv.at[color, seat(owner_f, owner_g)], moved(d, step),
                ).start()
            guarded([inside(d, step)], go)

    own = pltpu.make_async_copy(x_ref, buf.at[pl.ds(pl.multiple_of(me * rows, 8), rows)], own_sem)
    own.start()
    zero = (0,) * len(plan.dims)
    for stage in range(len(plan.dims)):
        for color, order in enumerate(plan.orders):
            moves = [m for m in plan.steps(zero, order) if m[0] == order[stage]]
            pass_on(color, piece(x_ref, 0, color), f, g, moves, [])
    if plan.core[1] == 2:
        for color in range(colors):
            remote(
                piece(x_ref, 0, color), buf, me * rows, color, side_send.at[color, seat(f, g)],
                side_recv.at[color, seat(f, g)], sibling,
            ).start()

    between()

    def owner_of(offset):
        owner_f, owner_g, conditions = f, g, []
        for d, (axis, stride, n) in enumerate(plan.dims):
            if not offset[d]:
                continue
            move = (1 - 2 * at[d]) if n == 2 else -offset[d]
            if n > 2:
                conditions.append(at[d] - offset[d] >= 0 if offset[d] > 0 else at[d] - offset[d] <= n - 1)
            if axis == "front":
                owner_f = owner_f + move * stride
            else:
                owner_g = owner_g + move * stride
        return owner_f, owner_g, conditions

    for color, offset in plan.items:
        owner_f, owner_g, conditions = owner_of(offset)

        def arrive(color=color, offset=offset, owner_f=owner_f, owner_g=owner_g):
            first = (owner_f * plan.grid + owner_g) * rows
            here = piece(buf, first, color)
            remote(here, buf, first, color, send.at[0, color, seat(f, g)], recv.at[color, seat(owner_f, owner_g)], sibling).wait_recv()
            pass_on(color, here, owner_f, owner_g, plan.steps(offset, plan.orders[color]), conditions)
            if plan.core[1] == 2:
                remote(
                    here, buf, first, color, side_send.at[color, seat(owner_f, owner_g)],
                    side_recv.at[color, seat(owner_f, owner_g)], sibling,
                ).start()

        guarded(conditions, arrive)

    def finish():
        own.wait()
        everything = [(color, zero) for color in range(colors)] + plan.items
        for color, offset in everything:
            owner_f, owner_g, conditions = owner_of(offset)

            def settle(color=color, offset=offset, owner_f=owner_f, owner_g=owner_g):
                first = (owner_f * plan.grid + owner_g) * rows
                here = piece(buf, first, color)
                for d, step in plan.steps(offset, plan.orders[color]):
                    def gone(d=d, step=step):
                        remote(
                            here, buf, first, color, send.at[lane(d, step), color, seat(owner_f, owner_g)],
                            recv.at[color, seat(owner_f, owner_g)], moved(d, step),
                        ).wait_send()
                    guarded([inside(d, step)], gone)
                if plan.core[1] == 2:
                    remote(
                        here, buf, first, color, side_send.at[color, seat(owner_f, owner_g)],
                        side_recv.at[color, seat(owner_f, owner_g)], sibling,
                    ).wait_send()
                    theirs = ((owner_f + 1 - 2 * lax.rem(owner_f, 2)) * plan.grid + owner_g) * rows
                    remote(
                        piece(buf, theirs, color), buf, theirs, color, side_send.at[color, seat(owner_f, owner_g)],
                        side_recv.at[color, seat(owner_f, owner_g)], sibling,
                    ).wait_recv()

            guarded(conditions, settle)

    return finish


def greet(plan, everyone=False):
    f, g = lax.axis_index("front"), lax.axis_index("grid")
    bar = pltpu.get_barrier_semaphore()
    if everyone:
        total = plan.front * plan.grid
        me = f * plan.grid + g
        def hello(i, c):
            t = lax.rem(me + i, total)
            pl.semaphore_signal(bar, inc=1, device_id=(t // plan.grid, lax.rem(t, plan.grid)), device_id_type=MESH)
            return c
        lax.fori_loop(1, total, hello, 0)
        pl.semaphore_wait(bar, total - 1)


def ag_scratch(plan):
    seats = plan.front * plan.grid // plan.core[1]
    colors = len(plan.orders)
    return [
        pltpu.SemaphoreType.DMA(()),
        pltpu.SemaphoreType.DMA((2 * len(plan.dims), colors, seats)),
        pltpu.SemaphoreType.DMA((colors, seats)),
        pltpu.SemaphoreType.DMA((colors, seats)),
        pltpu.SemaphoreType.DMA((colors, seats)),
    ]


def halves(a):
    high = a.astype(jnp.bfloat16)
    return high, (a - high.astype(jnp.float32)).astype(jnp.bfloat16)


def dot(a, b):
    return jnp.dot(a, b, preferred_element_type=jnp.float32)


def add_product(acc, a_ref, high, low, tile):
    for m in range(a_ref.shape[0] // tile):
        rows = pl.ds(m * tile, tile)
        a_high, a_low = halves(a_ref[rows, :])
        acc[rows, :] += dot(a_high, high) + (dot(a_low, high) + dot(a_high, low))


def flat(block):
    return jnp.concatenate([block[:, 0, :], block[:, 1, :]], axis=1)


class Mail:
    def __init__(self, plan, rows, own_rows):
        self.plan, self.rows, self.own_rows = plan, rows, own_rows
        self.devices = plan.front * plan.grid
        mean = rows / self.devices
        self.slots = max(8, math.ceil((mean + 4.2 * math.sqrt(mean)) / 8) * 8)
        self.total = self.devices * self.slots
        self.parts = next(p for p in (4, 2, 1) if self.total % (16 * p) == 0)
        self.part = self.total // self.parts

    def scratch(self):
        return [
            pltpu.VMEM((self.devices, self.rows), jnp.float32),
            pltpu.VMEM((1, self.rows), jnp.float32),
            pltpu.VMEM((self.total, 1), jnp.float32),
            pltpu.VMEM((self.rows, 512), jnp.bfloat16),
            pltpu.VMEM((self.total, 256), jnp.float32),
            pltpu.VMEM((self.total, 256), jnp.float32),
            pltpu.SemaphoreType.DMA(()),
            pltpu.SemaphoreType.DMA((self.devices,)),
            pltpu.SemaphoreType.DMA((self.devices,)),
        ]

    def address(self, where, shift, peak, key, slot, target):
        n, rows, own = self.devices, self.rows, self.own_rows
        me = lax.axis_index("front") * self.plan.grid + lax.axis_index("grid")
        before = lax.broadcasted_iota(jnp.int32, (rows, rows), 0) < lax.broadcasted_iota(jnp.int32, (rows, rows), 1)
        before = jnp.where(before, 1.0, 0.0).astype(jnp.bfloat16)
        block = lax.broadcasted_iota(jnp.int32, (n, rows), 0)
        mine = where[pl.ds(me, 1), :]
        sent = (mine >= block * own) & (mine < (block + 1) * own)
        places = where[...] - me * own
        got = (places >= 0) & (places < own)
        both = jnp.concatenate([jnp.where(sent, 1.0, 0.0), jnp.where(got, 1.0, 0.0)], axis=0)
        rank = dot(both.astype(jnp.bfloat16), before) - shift
        own_rank, got_rank = rank[:n], rank[n:]
        fits = sent & (own_rank >= 0) & (own_rank < self.slots)
        number = (block * self.slots).astype(jnp.float32) + own_rank + 1.0
        slot[...] = jnp.sum(jnp.where(fits, number, 0.0), axis=0, keepdims=True) - 1.0
        key[...] = jnp.where(got, got_rank, -1.0)
        counter = lax.broadcasted_iota(jnp.int32, (self.slots, rows), 0).astype(jnp.float32)
        first = (block * own)

        def one(s, most):
            which = where[pl.ds(s, 1), :]
            held = counter == key[pl.ds(s, 1), :]
            place = (which - me * own + 1).astype(jnp.float32)
            found = jnp.sum(jnp.where(held, place, 0.0), axis=1, keepdims=True) - 1.0
            target[pl.ds(pl.multiple_of(s * self.slots, 8), self.slots), :] = found
            inside = (which >= first) & (which < first + own)
            return jnp.maximum(most, jnp.sum(jnp.where(inside, 1.0, 0.0), axis=1, keepdims=True))

        most = lax.fori_loop(0, n, one, jnp.zeros((n, 1), jnp.float32))
        if peak is not None:
            peak[...] = jnp.broadcast_to(jnp.max(most, axis=0, keepdims=True), peak.shape)

    def pack(self, slot, pair, out):
        def one(p, c):
            base = p * self.part
            ids = (lax.broadcasted_iota(jnp.int32, (self.part, self.rows), 0) + base).astype(jnp.float32)
            chosen = jnp.where(ids == slot[...], 1.0, 0.0).astype(jnp.bfloat16)
            both = dot(chosen, pair[...])
            out[pl.ds(pl.multiple_of(base, 8), self.part), :] = both[:, :256] + both[:, 256:]
            return c
        lax.fori_loop(0, self.parts, one, 0)

    def peer(self, i):
        me = lax.axis_index("front") * self.plan.grid + lax.axis_index("grid")
        return lax.rem(me + i, self.devices)

    def letter(self, i, out, inbox, sent, received):
        t = self.peer(i)
        me = self.peer(0)
        rows = lambda ref, b: ref.at[pl.ds(pl.multiple_of(b * self.slots, 8), self.slots)]
        return pltpu.make_async_remote_copy(
            src_ref=rows(out, t), dst_ref=rows(inbox, me), send_sem=sent.at[i],
            recv_sem=received.at[i], device_id=(t // self.plan.grid, lax.rem(t, self.plan.grid)),
            device_id_type=MESH,
        )

    def home(self, out, inbox, sem):
        me = self.peer(0)
        rows = lambda ref: ref.at[pl.ds(pl.multiple_of(me * self.slots, 8), self.slots)]
        return pltpu.make_async_copy(rows(out), rows(inbox), sem)

    def send(self, out, inbox, sem, sent, received):
        self.home(out, inbox, sem).start()

        def one(i, c):
            self.letter(i, out, inbox, sent, received).start()
            return c
        lax.fori_loop(1, self.devices, one, 0)

    def settle(self, out, inbox, sem, sent, received):
        def one(i, c):
            self.letter(i, out, inbox, sent, received).wait()
            return c
        lax.fori_loop(1, self.devices, one, 0)
        self.home(out, inbox, sem).wait()

    def unpack(self, target, inbox, acc):
        def one(p, c):
            rows = pl.ds(pl.multiple_of(p * self.part, 8), self.part)
            places = lax.broadcasted_iota(jnp.int32, (self.part, self.own_rows), 1).astype(jnp.float32)
            chosen = jnp.where(target[rows, :] == places, 1.0, 0.0).astype(jnp.bfloat16)
            pair = jnp.concatenate(halves(inbox[rows, :]), axis=1)
            both = lax.dot_general(chosen, pair, (((0,), (0,)), ((), ())), preferred_element_type=jnp.float32)
            acc[...] += both[:, :256] + both[:, 256:]
            return c
        lax.fori_loop(0, self.parts, one, 0)


def main_kernel(plan, mail, index, live, x, u_hbm, f_hbm, out, sample, peak, rest_out, rows_all, where, child, ubuf,
                fbuf, acc, total, usem, fsem, wsem, wsend, wrecv, ssem, *more):
    ag, post = more[:5], more[5:]
    key, slot, target, pair, outbox, inbox, msem, sent, received = post
    f, g = lax.axis_index("front"), lax.axis_index("grid")
    greet(plan, True)
    depth, wide = child.shape[1], fbuf.shape[2]
    u_steps, f_steps = u_hbm.shape[1] // depth, f_hbm.shape[1] // wide
    slots = ubuf.shape[0]

    def u_copy(k):
        s = lax.rem(k, slots)
        return pltpu.make_async_copy(u_hbm.at[:, pl.ds(pl.multiple_of(k * depth, depth), depth)], ubuf.at[s], usem.at[s])

    def f_copy(k):
        s = lax.rem(k, slots)
        return pltpu.make_async_copy(f_hbm.at[:, pl.ds(pl.multiple_of(k * wide, wide), wide)], fbuf.at[s], fsem.at[s])

    block = plan.grid
    def here(ref, ff):
        return ref.at[pl.ds(pl.multiple_of(ff * block, 8), block)]
    def exchange(i):
        return pltpu.make_async_remote_copy(
            src_ref=live, dst_ref=here(where, f), send_sem=wsend.at[i], recv_sem=wrecv.at[i],
            device_id=(lax.rem(f + i, plan.front), g), device_id_type=MESH,
        )
    for i in range(1, plan.front):
        exchange(i).start()
    mine = pltpu.make_async_copy(live, here(where, f), wsem)
    mine.start()
    for k in range(slots):
        u_copy(k).start()
        f_copy(k).start()

    def between():
        for i in range(1, plan.front):
            exchange(i).wait()
        mine.wait()
        mail.address(where, 0.0, peak, key, slot, target)

    finish = gather_rows(plan, x, rows_all, *ag, between=between)
    finish()

    acc[...] = jnp.zeros_like(acc)

    def u_step(k, c):
        u_copy(k).wait()
        def fetch(j, c):
            for t in range(16):
                r = j * 16 + t
                child[0, r] = rows_all[index[k * depth + r]]
            return c
        lax.fori_loop(0, depth // 16, fetch, 0)
        high, low = halves(flat(child[0]))
        add_product(acc, ubuf.at[lax.rem(k, slots)], high, low, 256)
        @pl.when(k + slots < u_steps)
        def _():
            u_copy(k + slots).start()
        return c
    lax.fori_loop(0, u_steps, u_step, 0)

    pair[...] = jnp.concatenate(halves(acc[...]), axis=1)
    mail.pack(slot, pair, outbox)
    keep = pltpu.make_async_copy(acc, sample, ssem)
    keep.start()
    mail.send(outbox, inbox, msem, sent, received)

    total[...] = jnp.zeros_like(total)

    def f_step(k, c):
        f_copy(k).wait()
        high, low = halves(flat(rows_all[pl.ds(pl.multiple_of(k * wide, wide), wide)]))
        add_product(total, fbuf.at[lax.rem(k, slots)], high, low, min(256, fbuf.shape[1]))
        @pl.when(k + slots < f_steps)
        def _():
            f_copy(k + slots).start()
        return c
    lax.fori_loop(0, f_steps, f_step, 0)

    mail.settle(outbox, inbox, msem, sent, received)
    mail.unpack(target, inbox, total)
    out[...] = total[...]
    copy = pltpu.make_async_copy(where, rest_out, wsem)
    copy.start()
    copy.wait()
    keep.wait()


def extra_kernel(plan, mail, shift, where, sample, so_far, out, pair, *post):
    key, slot, target, pair2, outbox, inbox, msem, sent, received = post
    greet(plan, True)
    mail.address(where, shift[0:1, 0:1], None, key, slot, target)
    pair2[...] = jnp.concatenate(halves(sample[...]), axis=1)
    mail.pack(slot, pair2, outbox)
    mail.send(outbox, inbox, msem, sent, received)
    pair[...] = so_far[...]
    mail.settle(outbox, inbox, msem, sent, received)
    mail.unpack(target, inbox, pair)
    out[...] = pair[...]


def shards(plan, index_map, lengths, update_front, front_matrix, random):
    order, own_rows = index_map.shape[1], front_matrix.shape[0]
    rows, width = update_front.shape[1], random.shape[1]
    mail = Mail(plan, rows, own_rows)
    index = index_map[0]
    live = jnp.where(jnp.arange(order, dtype=jnp.int32) < lengths[0], index, -1).reshape(plan.grid, rows)
    x = random.reshape(own_rows, 2, width // 2)
    depth, wide, slots = 512, 1024, 3
    vmem, any_ = pl.BlockSpec(memory_space=pltpu.VMEM), pl.BlockSpec(memory_space=pl.ANY)
    devices = plan.front * plan.grid
    first, sample, peak, where = pl.pallas_call(
        functools.partial(main_kernel, plan, mail),
        out_shape=(
            jax.ShapeDtypeStruct((own_rows, width), jnp.float32),
            jax.ShapeDtypeStruct((rows, width), jnp.float32),
            jax.ShapeDtypeStruct((8, 128), jnp.float32),
            jax.ShapeDtypeStruct((devices, rows), jnp.int32),
        ),
        in_specs=[pl.BlockSpec(memory_space=pltpu.SMEM), vmem, vmem, any_, any_],
        out_specs=(vmem, any_, vmem, any_),
        scratch_shapes=[
            pltpu.VMEM((own_rows * devices, 2, width // 2), jnp.float32),
            pltpu.VMEM((devices, rows), jnp.int32),
            pltpu.VMEM((2, depth, 2, width // 2), jnp.float32),
            pltpu.VMEM((slots, rows, depth), jnp.float32),
            pltpu.VMEM((slots, own_rows, wide), jnp.float32),
            pltpu.VMEM((rows, width), jnp.float32),
            pltpu.VMEM((own_rows, width), jnp.float32),
            pltpu.SemaphoreType.DMA((slots,)),
            pltpu.SemaphoreType.DMA((slots,)),
            pltpu.SemaphoreType.DMA(()),
            pltpu.SemaphoreType.DMA((plan.front,)),
            pltpu.SemaphoreType.DMA((plan.front,)),
            pltpu.SemaphoreType.DMA(()),
            *ag_scratch(plan),
            *mail.scratch(),
        ],
        compiler_params=pltpu.CompilerParams(collective_id=0, has_side_effects=True, vmem_limit_bytes=63 << 20),
    )(index, live, x, update_front[0], front_matrix)

    def more(carry):
        done, so_far = carry
        shift = jnp.full((8, 128), done, jnp.float32)
        added = pl.pallas_call(
            functools.partial(extra_kernel, plan, mail),
            out_shape=jax.ShapeDtypeStruct((own_rows, width), jnp.float32),
            in_specs=[vmem] * 4,
            out_specs=vmem,
            scratch_shapes=[pltpu.VMEM((own_rows, width), jnp.float32), *mail.scratch()],
            compiler_params=pltpu.CompilerParams(collective_id=1, has_side_effects=True, vmem_limit_bytes=63 << 20),
        )(shift, where, sample, so_far)
        return done + mail.slots, added

    return lax.while_loop(lambda carry: carry[0] < peak[0, 0], more, (jnp.float32(mail.slots), first))[1]


def solution(mesh):
    plan = Plan(mesh)
    placed = (
        P("front", None),
        P("front"),
        P("front", "grid", None),
        P(("front", "grid"), None),
        P(("front", "grid"), None),
    )
    return jax.shard_map(
        functools.partial(shards, plan), mesh=mesh, in_specs=placed, out_specs=P(("front", "grid"), None),
        check_vma=False,
    )
```

time: 392 us -> 163 us (0.42)
  waiting for transfers between devices: 226 us -> 0 us
  Pallas kernels: 0 us -> 153 us
  matrix products: 100 us -> 0 us
  local copies, waits for them, and re-layouts: 40.2 us -> 4.68 us
  between operations: 13.8 us -> 0.67 us
  other arithmetic: 11.2 us -> 2.13 us
    all_gather x2 -> x0, waiting for transfers between devices: 218 us -> none  [the longest x1 118 us: shards(): lax.all_gather(random, ('front', 'grid'), axis=0, tiled=True)]
    pallas_call x0 -> x1, Pallas kernels: none -> 153 us  [shards(): pl.pallas_call(functools.partial(main_kernel, plan, mail), out_shape=(jax...]
    dot_general x4 -> x0, matrix products: 100 us -> none  [the longest x3 78.4 us: product(): jnp.dot(a, b, preferred_element_type=jnp.float32, precision=lax.Precision...]
    gather x1 -> x0, local copies, waits for them, and re-layouts: 37.3 us -> none  [shards(): child_random = jnp.take(gathered_random, index_rows, axis=0)]
    another operation x1 -> x0, other arithmetic: 8.15 us -> none
    reduce_scatter x1 -> x0, waiting for transfers between devices: 6.93 us -> none  [shards(): added = lax.psum_scatter(terms, 'front', scatter_dimension=0, tiled=True)[0]]
  transfers between devices with their start and end apart: 3 -> 0, of which waited for: 3 -> 0; matrix products, arithmetic and copies ran while one was open for 12% -> 0% of each run, Pallas kernels for 0% -> 0%
where the time goes in v1:
time: 163 us; the launch traced here: 161 us
  Pallas kernels  153 us (94%)
  local copies, waits for them, and re-layouts  4.68 us (3%)
  other arithmetic  2.13 us (1%)
    pallas_call x1, Pallas kernels, shards(): pl.pallas_call(functools.partial(main_kernel, plan, mail), out_shape=(jax...  153 us

profile of v1, /device:TPU:0, one launch (start us, length us, event | category | flops | bytes accessed | tf_op | source)
XLA Modules:
  0.0 161.3 jit_solution(16634030717392843303)
XLA Ops:
  0.0 2.1 %reshape.6.x = f32[512,2,128]{2,1,0:T(2,128)} reshape(f32[512,256]{1,0:T(8,128)} %param.11) | data formatting | bytes 1048576 | tf_op jit(solution)/shard_map/reshape | solution.py:463
  2.1 0.6 broadcast.7
  2.7 1.5 reduce.3
  4.9 0.6 fusion.live
  5.5 153.2 %shard_map.55 = (f32[512,256]{1,0:T(8,128)S(1)}, f32[1024,256]{1,0:T(8,128)}, f32[8,128]{1,0:T(8,128)}, s32[32,1024]{1,0:T(8,128)S(1)}) custom-call(s32[8192]{0:T(1024)} %bitcast.7, s32[8,1024]{1,0:T(8,128)} %fusion.live, f32[512,2,128]{2,1,0:T(2,128)} %reshape.6.x, f32[1024,8192]{1,0:T(8,128)} %bitcast.6, f32[512,16384]{1,0:T(8,128)} %f_hbm.1), custom_call_target="tpu_custom_call" | custom-call | tf_op jit(solution)/shard_map/pallas_call | solution.py:467
  158.7 1.8 %while.10 = (f32[]{:T(128)}, f32[512,256]{1,0:T(8,128)S(1)}, f32[8,128]{1,0:T(8,128)}, s32[32,1024]{1,0:T(8,128)S(1)}, f32[1024,256]{1,0:T(8,128)}, /*index=5*/f32[]{:T(128)}) while((f32[]{:T(128)}, f32[512,256]{1,0:T(8,128)S(1)}, f32[8,128]{1,0:T(8,128)}, s32[32,1024]{1,0:T(8,128)S(1)}, f32[1024,256]{1,0:T(8,128)}, /*index=5*/f32[]{:T(128)}) %tuple.18), condition=%wide.region_1.2_spmd, body=%wide.region_0.1_spmd.sunk | while | flops 2 | bytes 1052753 | solution.py:510
  158.7 1.2 slice.3
  160.5 0.8 copy.16
  (1 shorter events, 0.0 us)

commit v2 on v1

--- a/solution.py
+++ b/solution.py
@@ -66,7 +66,7 @@
         return [(color, offset) for hops, _, color, offset in items if hops]
 
 
-def gather_rows(plan, x_ref, buf, own_sem, send, side_send, recv, side_recv, between=lambda: None):
+def gather_rows(plan, x_ref, buf, own_sem, send, side_send, recv, side_recv, between=lambda: None, chores=()):
     f, g = lax.axis_index("front"), lax.axis_index("grid")
     rows = x_ref.shape[0]
     colors = len(plan.orders)
@@ -147,7 +147,11 @@
                 owner_g = owner_g + move * stride
         return owner_f, owner_g, conditions
 
-    for color, offset in plan.items:
+    done = 0
+    for number, (color, offset) in enumerate(plan.items):
+        while done * len(plan.items) < number * len(chores):
+            chores[done]()
+            done += 1
         owner_f, owner_g, conditions = owner_of(offset)
 
         def arrive(color=color, offset=offset, owner_f=owner_f, owner_g=owner_g):
@@ -162,6 +166,8 @@
                 ).start()
 
         guarded(conditions, arrive)
+    for chore in chores[done:]:
+        chore()
 
     def finish():
         own.wait()
@@ -256,7 +262,6 @@
             pltpu.VMEM((self.devices, self.rows), jnp.float32),
             pltpu.VMEM((1, self.rows), jnp.float32),
             pltpu.VMEM((self.total, 1), jnp.float32),
-            pltpu.VMEM((self.rows, 512), jnp.bfloat16),
             pltpu.VMEM((self.total, 256), jnp.float32),
             pltpu.VMEM((self.total, 256), jnp.float32),
             pltpu.SemaphoreType.DMA(()),
@@ -295,7 +300,7 @@
 
         most = lax.fori_loop(0, n, one, jnp.zeros((n, 1), jnp.float32))
         if peak is not None:
-            peak[...] = jnp.broadcast_to(jnp.max(most, axis=0, keepdims=True), peak.shape)
+            peak[0, 0] = jnp.max(most)
 
     def pack(self, slot, pair, out):
         def one(p, c):
@@ -353,39 +358,49 @@
         lax.fori_loop(0, self.parts, one, 0)
 
 
-def main_kernel(plan, mail, index, live, x, u_hbm, f_hbm, out, sample, peak, rest_out, rows_all, where, child, ubuf,
-                fbuf, acc, total, usem, fsem, wsem, wsend, wrecv, ssem, *more):
+def main_kernel(plan, mail, index, length, places, x, u_hbm, f_hbm, out, sample, peak, where_out, rows_all, x_rows, live,
+                where, child_a, child_b, u_high, u_low, tiles, acc, tsem, wsem, wsend, wrecv, ssem, *more):
     ag, post = more[:5], more[5:]
-    key, slot, target, pair, outbox, inbox, msem, sent, received = post
+    key, slot, target, outbox, inbox, msem, sent, received = post
     f, g = lax.axis_index("front"), lax.axis_index("grid")
+    ring, tall, wide = tiles.shape
+    rows, order = u_hbm.shape
+    half = x.shape[1] // 2
+    depth = child_a.shape[0]
+
+    def tile_copy(source, n, across):
+        r, k = n // across, lax.rem(n, across)
+        s = lax.rem(n, ring)
+        return pltpu.make_async_copy(
+            source.at[pl.ds(pl.multiple_of(r * tall, 8), tall), pl.ds(pl.multiple_of(k * wide, 128), wide)],
+            tiles.at[s], tsem.at[s],
+        )
+
+    u_across, f_across = order // wide, f_hbm.shape[1] // wide
+    u_tiles, f_tiles = rows // tall * u_across, f_hbm.shape[0] // tall * f_across
+    for n in range(ring):
+        tile_copy(u_hbm, n, u_across).start()
+    for h in range(2):
+        x_rows[:, h, :] = x[:, h * half : (h + 1) * half]
+    lane = lax.broadcasted_iota(jnp.int32, (1, rows), 1)
+    for s in range(plan.grid):
+        held = places[0:1, s * rows : (s + 1) * rows]
+        live[s : s + 1, :] = jnp.where(lane + s * rows < length[0], held, -1)
     greet(plan, True)
-    depth, wide = child.shape[1], fbuf.shape[2]
-    u_steps, f_steps = u_hbm.shape[1] // depth, f_hbm.shape[1] // wide
-    slots = ubuf.shape[0]
-
-    def u_copy(k):
-        s = lax.rem(k, slots)
-        return pltpu.make_async_copy(u_hbm.at[:, pl.ds(pl.multiple_of(k * depth, depth), depth)], ubuf.at[s], usem.at[s])
-
-    def f_copy(k):
-        s = lax.rem(k, slots)
-        return pltpu.make_async_copy(f_hbm.at[:, pl.ds(pl.multiple_of(k * wide, wide), wide)], fbuf.at[s], fsem.at[s])
-
-    block = plan.grid
+
     def here(ref, ff):
-        return ref.at[pl.ds(pl.multiple_of(ff * block, 8), block)]
+        return ref.at[pl.ds(pl.multiple_of(ff * plan.grid, 8), plan.grid)]
+
     def exchange(i):
         return pltpu.make_async_remote_copy(
             src_ref=live, dst_ref=here(where, f), send_sem=wsend.at[i], recv_sem=wrecv.at[i],
             device_id=(lax.rem(f + i, plan.front), g), device_id_type=MESH,
         )
+
     for i in range(1, plan.front):
         exchange(i).start()
     mine = pltpu.make_async_copy(live, here(where, f), wsem)
     mine.start()
-    for k in range(slots):
-        u_copy(k).start()
-        f_copy(k).start()
 
     def between():
         for i in range(1, plan.front):
@@ -393,97 +408,144 @@
         mine.wait()
         mail.address(where, 0.0, peak, key, slot, target)
 
-    finish = gather_rows(plan, x, rows_all, *ag, between=between)
+    def f_copy(n):
+        s = lax.rem(n + u_tiles, ring)
+        r, k = n // f_across, lax.rem(n, f_across)
+        return pltpu.make_async_copy(
+            f_hbm.at[pl.ds(pl.multiple_of(r * tall, 8), tall), pl.ds(pl.multiple_of(k * wide, 128), wide)],
+            tiles.at[s], tsem.at[s],
+        )
+
+    def split_tile(n):
+        def chore():
+            tile_copy(u_hbm, n, u_across).wait()
+            r, k = n // u_across * tall, n % u_across * wide
+
+            def some(i, c):
+                first = pl.multiple_of(i * 32, 32)
+                high, low = halves(tiles[n % ring, pl.ds(first, 32), :])
+                u_high[pl.ds(r + first, 32), k : k + wide] = high
+                u_low[pl.ds(r + first, 32), k : k + wide] = low
+                return c
+
+            lax.fori_loop(0, tall // 32, some, 0)
+            if n + ring < u_tiles:
+                tile_copy(u_hbm, n + ring, u_across).start()
+            else:
+                f_copy(n + ring - u_tiles).start()
+        return chore
+
+    finish = gather_rows(
+        plan, x_rows, rows_all, *ag, between=between, chores=[split_tile(n) for n in range(u_tiles)]
+    )
     finish()
 
+    def fetch(child, k, first, count):
+        for r in range(first, first + count):
+            child[r] = rows_all[index[0, k * depth + r]]
+
+    def multiply(child, k, following, ahead):
+        high, low = halves(flat(child[...]))
+        tile = min(256, rows)
+        count = rows // tile
+        columns = pl.ds(pl.multiple_of(k * depth, 128), depth)
+        for m in range(count):
+            part = pl.ds(m * tile, tile)
+            a_high = u_high[part, columns]
+            acc[part, :] += dot(a_high, high) + (dot(u_low[part, columns], high) + dot(a_high, low))
+            fetch(following, ahead, m * depth // count, depth // count)
+
     acc[...] = jnp.zeros_like(acc)
-
-    def u_step(k, c):
-        u_copy(k).wait()
-        def fetch(j, c):
-            for t in range(16):
-                r = j * 16 + t
-                child[0, r] = rows_all[index[k * depth + r]]
-            return c
-        lax.fori_loop(0, depth // 16, fetch, 0)
-        high, low = halves(flat(child[0]))
-        add_product(acc, ubuf.at[lax.rem(k, slots)], high, low, 256)
-        @pl.when(k + slots < u_steps)
-        def _():
-            u_copy(k + slots).start()
+    steps = order // depth
+
+    def first_rows(j, c):
+        for t in range(16):
+            child_a[j * 16 + t] = rows_all[index[0, j * 16 + t]]
         return c
-    lax.fori_loop(0, u_steps, u_step, 0)
-
+
+    lax.fori_loop(0, depth // 16, first_rows, 0)
+
+    def two(j, c):
+        multiply(child_a, 2 * j, child_b, 2 * j + 1)
+        multiply(child_b, 2 * j + 1, child_a, lax.rem(2 * j + 2, steps))
+        return c
+
+    lax.fori_loop(0, steps // 2, two, 0)
+
+    width = acc.shape[1]
+    pair = u_high.at[:, pl.ds(0, 2 * width)]
     pair[...] = jnp.concatenate(halves(acc[...]), axis=1)
     mail.pack(slot, pair, outbox)
     keep = pltpu.make_async_copy(acc, sample, ssem)
     keep.start()
     mail.send(outbox, inbox, msem, sent, received)
-
-    total[...] = jnp.zeros_like(total)
-
-    def f_step(k, c):
-        f_copy(k).wait()
+    copy = pltpu.make_async_copy(where, where_out, wsem)
+    copy.start()
+
+    out[...] = jnp.zeros_like(out)
+
+    def f_step(n, c):
+        f_copy(n).wait()
+        r, k = n // f_across, lax.rem(n, f_across)
         high, low = halves(flat(rows_all[pl.ds(pl.multiple_of(k * wide, wide), wide)]))
-        add_product(total, fbuf.at[lax.rem(k, slots)], high, low, min(256, fbuf.shape[1]))
-        @pl.when(k + slots < f_steps)
+        add_product(out.at[pl.ds(pl.multiple_of(r * tall, 8), tall)], tiles.at[lax.rem(n + u_tiles, ring)], high, low, min(256, tall))
+
+        @pl.when(n + ring < f_tiles)
         def _():
-            f_copy(k + slots).start()
+            f_copy(n + ring).start()
+
         return c
-    lax.fori_loop(0, f_steps, f_step, 0)
+
+    lax.fori_loop(0, f_tiles, f_step, 0)
 
     mail.settle(outbox, inbox, msem, sent, received)
-    mail.unpack(target, inbox, total)
-    out[...] = total[...]
-    copy = pltpu.make_async_copy(where, rest_out, wsem)
-    copy.start()
+    mail.unpack(target, inbox, out)
     copy.wait()
     keep.wait()
 
 
-def extra_kernel(plan, mail, shift, where, sample, so_far, out, pair, *post):
-    key, slot, target, pair2, outbox, inbox, msem, sent, received = post
+def extra_kernel(plan, mail, shift, where, sample, so_far, out, pair2, *post):
+    key, slot, target, outbox, inbox, msem, sent, received = post
     greet(plan, True)
     mail.address(where, shift[0:1, 0:1], None, key, slot, target)
     pair2[...] = jnp.concatenate(halves(sample[...]), axis=1)
     mail.pack(slot, pair2, outbox)
     mail.send(outbox, inbox, msem, sent, received)
-    pair[...] = so_far[...]
+    out[...] = so_far[...]
     mail.settle(outbox, inbox, msem, sent, received)
-    mail.unpack(target, inbox, pair)
-    out[...] = pair[...]
+    mail.unpack(target, inbox, out)
 
 
 def shards(plan, index_map, lengths, update_front, front_matrix, random):
     order, own_rows = index_map.shape[1], front_matrix.shape[0]
     rows, width = update_front.shape[1], random.shape[1]
     mail = Mail(plan, rows, own_rows)
-    index = index_map[0]
-    live = jnp.where(jnp.arange(order, dtype=jnp.int32) < lengths[0], index, -1).reshape(plan.grid, rows)
-    x = random.reshape(own_rows, 2, width // 2)
-    depth, wide, slots = 512, 1024, 3
+    depth, ring, tall, wide = 512, 3, min(512, rows, own_rows), 512
     vmem, any_ = pl.BlockSpec(memory_space=pltpu.VMEM), pl.BlockSpec(memory_space=pl.ANY)
+    smem = pl.BlockSpec(memory_space=pltpu.SMEM)
     devices = plan.front * plan.grid
     first, sample, peak, where = pl.pallas_call(
         functools.partial(main_kernel, plan, mail),
         out_shape=(
             jax.ShapeDtypeStruct((own_rows, width), jnp.float32),
             jax.ShapeDtypeStruct((rows, width), jnp.float32),
-            jax.ShapeDtypeStruct((8, 128), jnp.float32),
+            jax.ShapeDtypeStruct((1, 1), jnp.float32),
             jax.ShapeDtypeStruct((devices, rows), jnp.int32),
         ),
-        in_specs=[pl.BlockSpec(memory_space=pltpu.SMEM), vmem, vmem, any_, any_],
-        out_specs=(vmem, any_, vmem, any_),
+        in_specs=[smem, smem, vmem, vmem, any_, any_],
+        out_specs=(vmem, any_, smem, any_),
         scratch_shapes=[
             pltpu.VMEM((own_rows * devices, 2, width // 2), jnp.float32),
+            pltpu.VMEM((own_rows, 2, width // 2), jnp.float32),
+            pltpu.VMEM((plan.grid, rows), jnp.int32),
             pltpu.VMEM((devices, rows), jnp.int32),
-            pltpu.VMEM((2, depth, 2, width // 2), jnp.float32),
-            pltpu.VMEM((slots, rows, depth), jnp.float32),
-            pltpu.VMEM((slots, own_rows, wide), jnp.float32),
+            pltpu.VMEM((depth, 2, width // 2), jnp.float32),
+            pltpu.VMEM((depth, 2, width // 2), jnp.float32),
+            pltpu.VMEM((rows, order), jnp.bfloat16),
+            pltpu.VMEM((rows, order), jnp.bfloat16),
+            pltpu.VMEM((ring, tall, wide), jnp.float32),
             pltpu.VMEM((rows, width), jnp.float32),
-            pltpu.VMEM((own_rows, width), jnp.float32),
-            pltpu.SemaphoreType.DMA((slots,)),
-            pltpu.SemaphoreType.DMA((slots,)),
+            pltpu.SemaphoreType.DMA((ring,)),
             pltpu.SemaphoreType.DMA(()),
             pltpu.SemaphoreType.DMA((plan.front,)),
             pltpu.SemaphoreType.DMA((plan.front,)),
@@ -491,8 +553,8 @@
             *ag_scratch(plan),
             *mail.scratch(),
         ],
-        compiler_params=pltpu.CompilerParams(collective_id=0, has_side_effects=True, vmem_limit_bytes=63 << 20),
-    )(index, live, x, update_front[0], front_matrix)
+        compiler_params=pltpu.CompilerParams(collective_id=0, has_side_effects=True, vmem_limit_bytes=67043328),
+    )(index_map, lengths, index_map, random, update_front[0], front_matrix)
 
     def more(carry):
         done, so_far = carry
@@ -502,7 +564,7 @@
             out_shape=jax.ShapeDtypeStruct((own_rows, width), jnp.float32),
             in_specs=[vmem] * 4,
             out_specs=vmem,
-            scratch_shapes=[pltpu.VMEM((own_rows, width), jnp.float32), *mail.scratch()],
+            scratch_shapes=[pltpu.VMEM((rows, 2 * width), jnp.bfloat16), *mail.scratch()],
             compiler_params=pltpu.CompilerParams(collective_id=1, has_side_effects=True, vmem_limit_bytes=63 << 20),
         )(shift, where, sample, so_far)
         return done + mail.slots, added

time: 163 us -> 150 us (0.920)
  Pallas kernels: 153 us -> 145 us
  local copies, waits for them, and re-layouts: 4.68 us -> 1.87 us
  other arithmetic: 2.13 us -> 0 us
    pallas_call x1, Pallas kernels: 153 us -> 145 us  [shards(): pl.pallas_call(functools.partial(main_kernel, plan, mail), out_shape=(jax...]
    reshape x1 -> x0, local copies, waits for them, and re-layouts: 2.09 us -> none  [shards(): x = random.reshape(own_rows, 2, width // 2)]
where the time goes in v2:
time: 150 us; the launch traced here: 148 us
  Pallas kernels  145 us (97%)
  local copies, waits for them, and re-layouts  1.87 us (1%)
    pallas_call x1, Pallas kernels, shards(): pl.pallas_call(functools.partial(main_kernel, plan, mail), out_shape=(jax...  145 us

profile of v2, /device:TPU:0, one launch (start us, length us, event | category | flops | bytes accessed | tf_op | source)
XLA Modules:
  0.0 147.7 jit_solution(7176194067613083043)
XLA Ops:
  0.7 144.6 %shard_map.55 = (f32[512,256]{1,0:T(8,128)}, f32[1024,256]{1,0:T(8,128)}, f32[1,1]{1,0:T(1,128)}, s32[32,1024]{1,0:T(8,128)}) custom-call(s32[1,8192]{1,0:T(1,128)} %places.1, s32[1]{0:T(128)S(6)} %copy.14.length, s32[1,8192]{1,0:T(1,128)} %places.1, f32[512,256]{1,0:T(8,128)} %x.1, f32[1024,8192]{1,0:T(8,128)} %bitcast.3, f32[512,16384]{1,0:T(8,128)} %f_hbm.1), custom_call_target="tpu_custom_call" | custom-call | tf_op jit(solution)/shard_map/pallas_call | solution.py:527
  145.3 0.6 while.10
  145.8 1.9 %copy.16 = f32[512,256]{1,0:T(8,128)} copy(f32[512,256]{1,0:T(8,128)} %get-tuple-element.41) | data formatting | bytes 1048576

commit v3 on v2

v3 whole, which is shorter than its diff:
```python
import functools
import itertools
import math

import jax
import jax.numpy as jnp
from jax import lax
from jax.experimental import pallas as pl
from jax.experimental.pallas import tpu as pltpu
from jax.sharding import PartitionSpec as P

MESH = pl.DeviceIdType.MESH


def axis_dims(places):
    found = []
    for d in range(len(places[0])):
        values = [p[d] for p in places]
        size = len(set(values))
        if size > 1:
            stride = next(i for i, v in enumerate(values) if v != values[0])
            found.append((stride, size))
    found.sort(reverse=True)
    if math.prod(size for _, size in found) != len(places):
        found = [(1, len(places))]
    return found


class Plan:
    def __init__(self, mesh):
        self.front, self.grid = mesh.shape["front"], mesh.shape["grid"]
        place = lambda d: (*d.coords, d.core_on_chip)
        fronts = axis_dims([place(d) for d in mesh.devices[:, 0]])
        grids = axis_dims([place(d) for d in mesh.devices[0, :]])
        self.core = fronts[-1] if fronts[-1][1] == 2 else (1, 1)
        if self.core[1] == 2:
            fronts = fronts[:-1]
        dims = [("front", s, n) for s, n in fronts] + [("grid", s, n) for s, n in grids]
        long = max(range(len(dims)), key=lambda i: dims[i][2])
        rest = [i for i in range(len(dims)) if i != long]
        self.dims = dims
        a, b = rest, rest[::-1]
        if len(rest) == 2:
            self.orders = [[(a[0], long, a[1]), (long, *b)], [(b[0], long, b[1]), (long, *a)]]
        else:
            self.orders = [[(*a, long), (long, *b)], [(*b, long), (long, *a)]]
        self.lanes, self.lane_count = {}, 0
        for d, (_, _, n) in enumerate(dims):
            for step in (1,) if n == 2 else (1, -1):
                self.lanes[d, step] = self.lane_count
                self.lane_count += 1
        self.items = [self.schedule(h) for h in range(2)]

    def steps(self, offset, order):
        last = max((i for i, d in enumerate(order) if offset[d]), default=-1)
        moves = []
        if last >= 0 and self.dims[order[last]][2] > 2:
            moves.append((order[last], 1 if offset[order[last]] > 0 else -1))
        for d in order[last + 1 :]:
            moves += [(d, 1)] if self.dims[d][2] == 2 else [(d, 1), (d, -1)]
        return moves

    def schedule(self, h):
        spans = [range(2) if n == 2 else range(1 - n, n) for _, _, n in self.dims]
        items = []
        for offset in itertools.product(*spans):
            for color, order in enumerate(self.orders[h]):
                stage = max((i for i, d in enumerate(order) if offset[d]), default=-1)
                items.append((sum(map(abs, offset)), stage, color, offset))
        items.sort()
        return [(color, offset) for hops, _, color, offset in items if hops]


class Gather:
    def __init__(self, plan, x_ref, buf, own_sem, send, side_send, recv, side_recv):
        self.plan, self.x_ref, self.buf, self.own_sem = plan, x_ref, buf, own_sem
        self.send, self.side_send, self.recv, self.side_recv = send, side_send, recv, side_recv
        self.f, self.g = f, g = lax.axis_index("front"), lax.axis_index("grid")
        self.rows, self.width = x_ref.shape[0], buf[0].shape[1]
        self.colors = len(plan.orders[0])
        self.part = self.rows // self.colors
        self.at = [lax.rem((f if axis == "front" else g) // s, n) for axis, s, n in plan.dims]
        self.sibling = (f + 1 - 2 * lax.rem(f, 2), g)
        self.zero = (0,) * len(plan.dims)

    def moved(self, d, step):
        axis, stride, n = self.plan.dims[d]
        move = (1 - 2 * self.at[d]) if n == 2 else step
        return (self.f + move * stride, self.g) if axis == "front" else (self.f, self.g + move * stride)

    def inside(self, d, step):
        n = self.plan.dims[d][2]
        if n == 2:
            return None
        return self.at[d] + step <= n - 1 if step > 0 else self.at[d] + step >= 0

    def guarded(self, conditions, body):
        conditions = [c for c in conditions if c is not None]
        if conditions:
            pl.when(functools.reduce(jnp.logical_and, conditions))(body)
        else:
            body()

    def here(self, owner_f, owner_g, h, color):
        first = (owner_f * self.plan.grid + owner_g) * self.rows + color * self.part
        return self.buf[h].at[pl.ds(pl.multiple_of(first, 8), self.part)]

    def given(self, h, color):
        return self.x_ref.at[pl.ds(color * self.part, self.part), pl.ds(h * self.width, self.width)]

    def seat(self, owner_f, owner_g):
        return (owner_f // self.plan.core[1]) * self.plan.grid + owner_g

    def hop(self, source, owner_f, owner_g, h, color, d, step):
        seat = self.seat(owner_f, owner_g)
        return pltpu.make_async_remote_copy(
            src_ref=source, dst_ref=self.here(owner_f, owner_g, h, color),
            send_sem=self.send.at[h, self.plan.lanes[d, step], color, seat], recv_sem=self.recv.at[h, color, seat],
            device_id=self.moved(d, step), device_id_type=MESH,
        )

    def aside(self, source, owner_f, owner_g, h, color):
        seat = self.seat(owner_f, owner_g)
        return pltpu.make_async_remote_copy(
            src_ref=source, dst_ref=self.here(owner_f, owner_g, h, color), send_sem=self.side_send.at[h, color, seat],
            recv_sem=self.side_recv.at[h, color, seat], device_id=self.sibling, device_id_type=MESH,
        )

    def pass_on(self, source, owner_f, owner_g, h, color, moves):
        for d, step in moves:
            self.guarded([self.inside(d, step)], self.hop(source, owner_f, owner_g, h, color, d, step).start)

    def own(self, h):
        block = pl.ds(pl.multiple_of((self.f * self.plan.grid + self.g) * self.rows, 8), self.rows)
        return pltpu.make_async_copy(
            self.x_ref.at[:, pl.ds(h * self.width, self.width)], self.buf[h].at[block], self.own_sem.at[h]
        )

    def begin(self, h):
        self.own(h).start()
        for stage in range(len(self.plan.dims)):
            for color, order in enumerate(self.plan.orders[h]):
                moves = [m for m in self.plan.steps(self.zero, order) if m[0] == order[stage]]
                self.pass_on(self.given(h, color), self.f, self.g, h, color, moves)
        if self.plan.core[1] == 2:
            for color in range(self.colors):
                self.aside(self.given(h, color), self.f, self.g, h, color).start()

    def owner_of(self, offset):
        owner_f, owner_g, conditions = self.f, self.g, []
        for d, (axis, stride, n) in enumerate(self.plan.dims):
            if not offset[d]:
                continue
            move = (1 - 2 * self.at[d]) if n == 2 else -offset[d]
            if n > 2:
                conditions.append(self.at[d] >= offset[d] if offset[d] > 0 else self.at[d] - offset[d] <= n - 1)
            if axis == "front":
                owner_f = owner_f + move * stride
            else:
                owner_g = owner_g + move * stride
        return owner_f, owner_g, conditions

    def arrive(self, h, color, offset):
        owner_f, owner_g, conditions = self.owner_of(offset)

        def body():
            here = self.here(owner_f, owner_g, h, color)
            self.hop(here, owner_f, owner_g, h, color, 0, 1).wait_recv()
            self.pass_on(here, owner_f, owner_g, h, color, self.plan.steps(offset, self.plan.orders[h][color]))
            if self.plan.core[1] == 2:
                self.aside(here, owner_f, owner_g, h, color).start()

        self.guarded(conditions, body)

    def every(self, h, body):
        for color, offset in [(color, self.zero) for color in range(self.colors)] + self.plan.items[h]:
            owner_f, owner_g, conditions = self.owner_of(offset)
            self.guarded(conditions, functools.partial(body, h, color, offset, owner_f, owner_g))

    def complete(self, h):
        self.own(h).wait()

        def body(h, color, offset, owner_f, owner_g):
            theirs = owner_f + 1 - 2 * lax.rem(owner_f, 2)
            self.aside(self.here(theirs, owner_g, h, color), theirs, owner_g, h, color).wait_recv()

        if self.plan.core[1] == 2:
            self.every(h, body)

    def drain(self, h):
        def body(h, color, offset, owner_f, owner_g):
            here = self.here(owner_f, owner_g, h, color)
            for d, step in self.plan.steps(offset, self.plan.orders[h][color]):
                self.guarded([self.inside(d, step)], self.hop(here, owner_f, owner_g, h, color, d, step).wait_send)
            if self.plan.core[1] == 2:
                self.aside(here, owner_f, owner_g, h, color).wait_send()

        self.every(h, body)


def greet(plan, everyone=False):
    f, g = lax.axis_index("front"), lax.axis_index("grid")
    bar = pltpu.get_barrier_semaphore()
    if everyone:
        total = plan.front * plan.grid
        me = f * plan.grid + g
        def hello(i, c):
            t = lax.rem(me + i, total)
            pl.semaphore_signal(bar, inc=1, device_id=(t // plan.grid, lax.rem(t, plan.grid)), device_id_type=MESH)
            return c
        lax.fori_loop(1, total, hello, 0)
        pl.semaphore_wait(bar, total - 1)


def ag_scratch(plan):
    seats = plan.front * plan.grid // plan.core[1]
    colors = len(plan.orders[0])
    return [
        pltpu.SemaphoreType.DMA((2,)),
        pltpu.SemaphoreType.DMA((2, plan.lane_count, colors, seats)),
        pltpu.SemaphoreType.DMA((2, colors, seats)),
        pltpu.SemaphoreType.DMA((2, colors, seats)),
        pltpu.SemaphoreType.DMA((2, colors, seats)),
    ]


def halves(a):
    high = a.astype(jnp.bfloat16)
    return high, (a - high.astype(jnp.float32)).astype(jnp.bfloat16)


def dot(a, b):
    return jnp.dot(a, b, preferred_element_type=jnp.float32)


def add_product(acc, a_ref, high, low, tile):
    for m in range(a_ref.shape[0] // tile):
        rows = pl.ds(m * tile, tile)
        a_high, a_low = halves(a_ref[rows, :])
        acc[rows, :] += dot(a_high, high) + (dot(a_low, high) + dot(a_high, low))


class Mail:
    def __init__(self, plan, rows, own_rows, width):
        self.plan, self.rows, self.own_rows, self.width = plan, rows, own_rows, width
        self.devices = plan.front * plan.grid
        mean = rows / self.devices
        self.slots = max(8, math.ceil((mean + 4.2 * math.sqrt(mean)) / 8) * 8)
        self.total = self.devices * self.slots
        self.parts = next(p for p in (4, 2, 1) if self.total % (16 * p) == 0)
        self.part = self.total // self.parts

    def scratch(self):
        return [
            pltpu.VMEM((self.devices, self.rows), jnp.float32),
            pltpu.VMEM((1, self.rows), jnp.float32),
            pltpu.VMEM((self.total, 1), jnp.float32),
            pltpu.VMEM((2, self.total, self.width), jnp.float32),
            pltpu.VMEM((2, self.total, self.width), jnp.float32),
            pltpu.SemaphoreType.DMA((2,)),
            pltpu.SemaphoreType.DMA((2, self.devices)),
            pltpu.SemaphoreType.DMA((2, self.devices)),
        ]

    def address(self, where, shift, peak, key, slot, target):
        n, rows, own = self.devices, self.rows, self.own_rows
        me = lax.axis_index("front") * self.plan.grid + lax.axis_index("grid")
        before = lax.broadcasted_iota(jnp.int32, (rows, rows), 0) < lax.broadcasted_iota(jnp.int32, (rows, rows), 1)
        before = jnp.where(before, 1.0, 0.0).astype(jnp.bfloat16)
        block = lax.broadcasted_iota(jnp.int32, (n, rows), 0)
        mine = where[pl.ds(me, 1), :]
        sent = (mine >= block * own) & (mine < (block + 1) * own)
        places = where[...] - me * own
        got = (places >= 0) & (places < own)
        both = jnp.concatenate([jnp.where(sent, 1.0, 0.0), jnp.where(got, 1.0, 0.0)], axis=0)
        rank = dot(both.astype(jnp.bfloat16), before) - shift
        own_rank, got_rank = rank[:n], rank[n:]
        fits = sent & (own_rank >= 0) & (own_rank < self.slots)
        number = (block * self.slots).astype(jnp.float32) + own_rank + 1.0
        slot[...] = jnp.sum(jnp.where(fits, number, 0.0), axis=0, keepdims=True) - 1.0
        key[...] = jnp.where(got, got_rank, -1.0)
        counter = lax.broadcasted_iota(jnp.int32, (self.slots, rows), 0).astype(jnp.float32)
        first = (block * own)

        def one(s, most):
            which = where[pl.ds(s, 1), :]
            held = counter == key[pl.ds(s, 1), :]
            place = (which - me * own + 1).astype(jnp.float32)
            found = jnp.sum(jnp.where(held, place, 0.0), axis=1, keepdims=True) - 1.0
            target[pl.ds(pl.multiple_of(s * self.slots, 8), self.slots), :] = found
            inside = (which >= first) & (which < first + own)
            return jnp.maximum(most, jnp.sum(jnp.where(inside, 1.0, 0.0), axis=1, keepdims=True))

        most = lax.fori_loop(0, n, one, jnp.zeros((n, 1), jnp.float32))
        if peak is not None:
            peak[0, 0] = jnp.max(most)

    def pack(self, slot, pair, out):
        def one(p, c):
            base = p * self.part
            ids = (lax.broadcasted_iota(jnp.int32, (self.part, self.rows), 0) + base).astype(jnp.float32)
            chosen = jnp.where(ids == slot[...], 1.0, 0.0).astype(jnp.bfloat16)
            both = dot(chosen, pair[...])
            out[pl.ds(pl.multiple_of(base, 8), self.part), :] = both[:, : self.width] + both[:, self.width :]
            return c
        lax.fori_loop(0, self.parts, one, 0)

    def peer(self, i):
        me = lax.axis_index("front") * self.plan.grid + lax.axis_index("grid")
        return lax.rem(me + i, self.devices)

    def letter(self, h, i, out, inbox, sent, received):
        t = self.peer(i)
        me = self.peer(0)
        rows = lambda ref, b: ref.at[h, pl.ds(pl.multiple_of(b * self.slots, 8), self.slots)]
        return pltpu.make_async_remote_copy(
            src_ref=rows(out, t), dst_ref=rows(inbox, me), send_sem=sent.at[h, i],
            recv_sem=received.at[h, i], device_id=(t // self.plan.grid, lax.rem(t, self.plan.grid)),
            device_id_type=MESH,
        )

    def home(self, h, out, inbox, sem):
        me = self.peer(0)
        rows = lambda ref: ref.at[h, pl.ds(pl.multiple_of(me * self.slots, 8), self.slots)]
        return pltpu.make_async_copy(rows(out), rows(inbox), sem.at[h])

    def send(self, h, out, inbox, sem, sent, received):
        self.home(h, out, inbox, sem).start()

        def one(i, c):
            self.letter(h, i, out, inbox, sent, received).start()
            return c
        lax.fori_loop(1, self.devices, one, 0)

    def settle(self, h, out, inbox, sem, sent, received):
        def one(i, c):
            self.letter(h, i, out, inbox, sent, received).wait()
            return c
        lax.fori_loop(1, self.devices, one, 0)
        self.home(h, out, inbox, sem).wait()

    def unpack(self, target, inbox, acc):
        def one(p, c):
            rows = pl.ds(pl.multiple_of(p * self.part, 8), self.part)
            places = lax.broadcasted_iota(jnp.int32, (self.part, self.own_rows), 1).astype(jnp.float32)
            chosen = jnp.where(target[rows, :] == places, 1.0, 0.0).astype(jnp.bfloat16)
            pair = jnp.concatenate(halves(inbox[rows, :]), axis=1)
            both = lax.dot_general(chosen, pair, (((0,), (0,)), ((), ())), preferred_element_type=jnp.float32)
            acc[...] += both[:, : self.width] + both[:, self.width :]
            return c
        lax.fori_loop(0, self.parts, one, 0)


def main_kernel(plan, mail, index, length, places, x, u_hbm, f_hbm, out, sample, peak, where_out, rows_0, rows_1, live,
                where, child, both, u_high, u_low, tiles, acc, product, pair, tsem, wsem, wsend, wrecv, ssem, *more):
    ag, post = more[:5], more[5:]
    key, slot, target, outbox, inbox, msem, sent, received = post
    f, g = lax.axis_index("front"), lax.axis_index("grid")
    ring, tall, wide = tiles.shape
    rows, order = u_hbm.shape
    rows_all = (rows_0, rows_1)
    width = rows_0.shape[1]
    depth = child.shape[0]
    gather = Gather(plan, x, rows_all, *ag)

    def tile_copy(source, n, across):
        r, k = n // across, n % across
        s = n % ring
        return pltpu.make_async_copy(
            source.at[pl.ds(r * tall, tall), pl.ds(k * wide, wide)], tiles.at[s], tsem.at[s]
        )

    u_across, f_across = order // wide, f_hbm.shape[1] // wide
    u_tiles, f_tiles = rows // tall * u_across, f_hbm.shape[0] // tall * f_across
    for n in range(ring):
        tile_copy(u_hbm, n, u_across).start()
    lane = lax.broadcasted_iota(jnp.int32, (1, rows), 1)
    for s in range(plan.grid):
        held = places[0:1, s * rows : (s + 1) * rows]
        live[s : s + 1, :] = jnp.where(lane + s * rows < length[0], held, -1)
    greet(plan, True)
    gather.begin(0)

    def here(ref, ff):
        return ref.at[pl.ds(pl.multiple_of(ff * plan.grid, 8), plan.grid)]

    def exchange(i):
        return pltpu.make_async_remote_copy(
            src_ref=live, dst_ref=here(where, f), send_sem=wsend.at[i], recv_sem=wrecv.at[i],
            device_id=(lax.rem(f + i, plan.front), g), device_id_type=MESH,
        )

    for i in range(1, plan.front):
        exchange(i).start()
    mine = pltpu.make_async_copy(live, here(where, f), wsem)
    mine.start()

    def f_copy(n):
        s = lax.rem(n + u_tiles, ring)
        r, k = n // f_across, lax.rem(n, f_across)
        return pltpu.make_async_copy(
            f_hbm.at[pl.ds(pl.multiple_of(r * tall, 8), tall), pl.ds(pl.multiple_of(k * wide, 128), wide)],
            tiles.at[s], tsem.at[s],
        )

    def split_tile(n):
        def chore():
            tile_copy(u_hbm, n, u_across).wait()
            r, k = n // u_across * tall, n % u_across * wide

            def some(i, c):
                first = pl.multiple_of(i * 32, 32)
                high, low = halves(tiles[n % ring, pl.ds(first, 32), :])
                u_high[pl.ds(r + first, 32), k : k + wide] = high
                u_low[pl.ds(r + first, 32), k : k + wide] = low
                return c

            lax.fori_loop(0, tall // 32, some, 0)
            if n + ring < u_tiles:
                tile_copy(u_hbm, n + ring, u_across).start()
            else:
                f_copy(n + ring - u_tiles).start()
        return chore

    def address():
        for i in range(1, plan.front):
            exchange(i).wait()
        mine.wait()
        mail.address(where, 0.0, peak, key, slot, target)
        pltpu.make_async_copy(where, where_out, wsem).start()

    steps = order // depth
    block = min(256, rows)
    blocks = rows // block

    def first_rows(h):
        def some(j, c):
            for t in range(16):
                child[pl.ds(j * 16 + t, 1), :] = rows_all[h][pl.ds(index[0, j * 16 + t], 1), :]
            return c
        lax.fori_loop(0, depth // 16, some, 0)

    def multiply(h, k):
        high, low = halves(child[...])
        both[:, :width] = high
        both[:, width:] = low
        columns = pl.ds(pl.multiple_of(k * depth, 128), depth)
        ahead = lax.rem(k + 1, steps) * depth
        count = depth // blocks
        for m in range(blocks):
            part = pl.ds(m * block, block)
            first = dot(u_high[part, columns], both[...])
            second = dot(u_low[part, columns], both[:, :width])
            acc[part, width:] += first[:, width:]
            acc[part, :width] += first[:, :width] + second
            for r in range(m * count, (m + 1) * count):
                child[pl.ds(r, 1), :] = rows_all[h][pl.ds(index[0, ahead + r], 1), :]

    def start_half(h):
        acc[...] = jnp.zeros_like(acc)
        first_rows(h)

    def keep(h):
        return pltpu.make_async_copy(product.at[h], sample.at[h], ssem.at[h])

    def post_half(h):
        product[h] = acc[:, :width] + acc[:, width:]
        high, low = halves(product[h])
        pair[:, :width] = high
        pair[:, width:] = low
        mail.pack(slot, pair, outbox.at[h])
        keep(h).start()
        mail.send(h, outbox, inbox, msem, sent, received)

    def run(h, chores):
        done = 0
        items = plan.items[h]
        for number, (color, offset) in enumerate(items):
            while done * len(items) < number * len(chores):
                chores[done]()
                done += 1
            gather.arrive(h, color, offset)
        for chore in chores[done:]:
            chore()

    chores = [address] + [split_tile(n) for n in range(u_tiles)]
    chores.insert(len(chores) * 3 // 4, lambda: gather.begin(1))
    run(0, chores)
    gather.complete(0)
    start_half(0)
    run(1, [functools.partial(multiply, 0, k) for k in range(steps)])
    post_half(0)
    gather.complete(1)
    start_half(1)

    def step(k, c):
        multiply(1, k)
        return c

    lax.fori_loop(0, steps, step, 0)
    post_half(1)

    out[...] = jnp.zeros_like(out)

    def f_step(n, c):
        f_copy(n).wait()
        r, k = n // f_across, lax.rem(n, f_across)
        at = pl.ds(pl.multiple_of(k * wide, wide), wide)
        high, low = halves(jnp.concatenate([rows_0[at, :], rows_1[at, :]], axis=1))
        add_product(out.at[pl.ds(pl.multiple_of(r * tall, 8), tall)], tiles.at[lax.rem(n + u_tiles, ring)], high, low, min(256, tall))

        @pl.when(n + ring < f_tiles)
        def _():
            f_copy(n + ring).start()

        return c

    lax.fori_loop(0, f_tiles, f_step, 0)
    gather.drain(0)
    gather.drain(1)
    for h in range(2):
        mail.settle(h, outbox, inbox, msem, sent, received)
        mail.unpack(target, inbox.at[h], out.at[:, pl.ds(h * width, width)])
    pltpu.make_async_copy(where, where_out, wsem).wait()
    for h in range(2):
        keep(h).wait()


def extra_kernel(plan, mail, shift, where, sample, so_far, out, pair, *post):
    key, slot, target, outbox, inbox, msem, sent, received = post
    width = mail.width
    greet(plan, True)
    mail.address(where, shift[0:1, 0:1], None, key, slot, target)
    for h in range(2):
        high, low = halves(sample[h])
        pair[:, :width] = high
        pair[:, width:] = low
        mail.pack(slot, pair, outbox.at[h])
        mail.send(h, outbox, inbox, msem, sent, received)
    out[...] = so_far[...]
    for h in range(2):
        mail.settle(h, outbox, inbox, msem, sent, received)
        mail.unpack(target, inbox.at[h], out.at[:, pl.ds(h * width, width)])


def shards(plan, index_map, lengths, update_front, front_matrix, random):
    order, own_rows = index_map.shape[1], front_matrix.shape[0]
    rows, width = update_front.shape[1], random.shape[1]
    half = width // 2
    mail = Mail(plan, rows, own_rows, half)
    depth, ring, tall, wide = 512, 3, min(512, rows, own_rows), 512
    vmem, any_ = pl.BlockSpec(memory_space=pltpu.VMEM), pl.BlockSpec(memory_space=pl.ANY)
    smem = pl.BlockSpec(memory_space=pltpu.SMEM)
    devices = plan.front * plan.grid
    first, sample, peak, where = pl.pallas_call(
        functools.partial(main_kernel, plan, mail),
        out_shape=(
            jax.ShapeDtypeStruct((own_rows, width), jnp.float32),
            jax.ShapeDtypeStruct((2, rows, half), jnp.float32),
            jax.ShapeDtypeStruct((1, 1), jnp.float32),
            jax.ShapeDtypeStruct((devices, rows), jnp.int32),
        ),
        in_specs=[smem, smem, vmem, vmem, any_, any_],
        out_specs=(vmem, any_, smem, any_),
        scratch_shapes=[
            pltpu.VMEM((own_rows * devices, half), jnp.float32),
            pltpu.VMEM((own_rows * devices, half), jnp.float32),
            pltpu.VMEM((plan.grid, rows), jnp.int32),
            pltpu.VMEM((devices, rows), jnp.int32),
            pltpu.VMEM((depth, half), jnp.float32),
            pltpu.VMEM((depth, width), jnp.bfloat16),
            pltpu.VMEM((rows, order), jnp.bfloat16),
            pltpu.VMEM((rows, order), jnp.bfloat16),
            pltpu.VMEM((ring, tall, wide), jnp.float32),
            pltpu.VMEM((rows, width), jnp.float32),
            pltpu.VMEM((2, rows, half), jnp.float32),
            pltpu.VMEM((rows, width), jnp.bfloat16),
            pltpu.SemaphoreType.DMA((ring,)),
            pltpu.SemaphoreType.DMA(()),
            pltpu.SemaphoreType.DMA((plan.front,)),
            pltpu.SemaphoreType.DMA((plan.front,)),
            pltpu.SemaphoreType.DMA((2,)),
            *ag_scratch(plan),
            *mail.scratch(),
        ],
        compiler_params=pltpu.CompilerParams(collective_id=0, has_side_effects=True, vmem_limit_bytes=67043328),
    )(index_map, lengths, index_map, random, update_front[0], front_matrix)

    def more(carry):
        done, so_far = carry
        shift = jnp.full((8, 128), done, jnp.float32)
        added = pl.pallas_call(
            functools.partial(extra_kernel, plan, mail),
            out_shape=jax.ShapeDtypeStruct((own_rows, width), jnp.float32),
            in_specs=[vmem] * 4,
            out_specs=vmem,
            scratch_shapes=[pltpu.VMEM((rows, width), jnp.bfloat16), *mail.scratch()],
            compiler_params=pltpu.CompilerParams(collective_id=1, has_side_effects=True, vmem_limit_bytes=63 << 20),
        )(shift, where, sample, so_far)
        return done + mail.slots, added

    return lax.while_loop(lambda carry: carry[0] < peak[0, 0], more, (jnp.float32(mail.slots), first))[1]


def solution(mesh):
    plan = Plan(mesh)
    placed = (
        P("front", None),
        P("front"),
        P("front", "grid", None),
        P(("front", "grid"), None),
        P(("front", "grid"), None),
    )
    return jax.shard_map(
        functools.partial(shards, plan), mesh=mesh, in_specs=placed, out_specs=P(("front", "grid"), None),
        check_vma=False,
    )
```

time: 150 us -> 139 us (0.927); the launches traced: 148 us -> 139 us
  Pallas kernels: 145 us -> 136 us
    pallas_call x1, Pallas kernels: 145 us -> 136 us  [shards(): pl.pallas_call(functools.partial(main_kernel, plan, mail), out_shape=(jax...]
where the time goes in v3:
time: 139 us
  Pallas kernels  136 us (98%)
  local copies, waits for them, and re-layouts  1.87 us (1%)
    pallas_call x1, Pallas kernels, shards(): pl.pallas_call(functools.partial(main_kernel, plan, mail), out_shape=(jax...  136 us

profile of v3, /device:TPU:0, one launch (start us, length us, event | category | flops | bytes accessed | tf_op | source)
XLA Modules:
  0.0 138.8 jit_solution(17011165907618007392)
XLA Ops:
  0.7 135.7 %shard_map.55 = (f32[512,256]{1,0:T(8,128)}, f32[2,1024,128]{2,1,0:T(8,128)}, f32[1,1]{1,0:T(1,128)}, s32[32,1024]{1,0:T(8,128)}) custom-call(s32[1,8192]{1,0:T(1,128)} %places.1, s32[1]{0:T(128)S(6)} %copy.14.length, s32[1,8192]{1,0:T(1,128)} %places.1, f32[512,256]{1,0:T(8,128)} %x.1, f32[1024,8192]{1,0:T(8,128)} %bitcast.3, f32[512,16384]{1,0:T(8,128)} %f_hbm.1), custom_call_target="tpu_custom_call" | custom-call | tf_op jit(solution)/shard_map/pallas_call | solution.py:555
  136.3 0.6 while.10
  136.9 1.9 %copy.16 = f32[512,256]{1,0:T(8,128)} copy(f32[512,256]{1,0:T(8,128)} %get-tuple-element.41) | data formatting | bytes 1048576
